TPU v7x, 32 devices: a whole 2x2x4 slice. The times are simulated.
32 devices in a mesh: tm: 8 (over y, x, core), cell: 4 (over z).
Axes of the slice: x: 2, y: 2, z: 4, core: 2. Of those that a mesh axis runs over, the one named last changes fastest.
Arguments:
- anomalies: bfloat16 [24, 2, 8192, 256], P('tm', None, 'cell'), may hold values from -6 to 6
- obs_cells: int32 [24, 128], P('tm', 'cell'), may hold values from 0 to 8191, as said below
- obs_counts: int32 [24, 4], P('tm', 'cell'), may hold values from 16 to 32
- obs_precision: float32 [24, 128], P('tm', 'cell'), may hold values from 0.1 to 1
- inflation: float32 [24], P('tm'), may hold values from 1 to 1.12
Outputs:
- smoothed: bfloat16 [24, 2, 8192, 256], P('tm', None, 'cell')
Inputs may be any that keep to these rules, and one draw needn't show every extreme that they name: `obs_cells`: slot k of a window names a cell of the block of 2048 cells that starts at (k // 32) * 2048; two slots may name the same cell.
All inputs are finite; a program needn't handle non-finite values.
Results may differ from a plain program's by a relative error of at most 0.017.
Values may be sent and summed in bfloat16 or wider, within the bound.
A program may use at most 128 MiB of HBM per device.

v0:
```python
import jax
import jax.numpy as jnp
from jax import lax
from jax.sharding import PartitionSpec as P


def matmul_f32(left, right):
    return jnp.dot(left, right, precision=lax.Precision.HIGHEST, preferred_element_type=jnp.float32)


def gram_of(picked, weights):
    as_float = picked.astype(jnp.float32)
    weighted = as_float * weights[:, :, None]
    return jnp.einsum(
        "wkm,wkn->wmn",
        weighted,
        as_float,
        precision=lax.Precision.HIGHEST,
        preferred_element_type=jnp.float32,
    )


def transform_of(gram, rho):
    members = gram.shape[-1]
    unit_matrix = jnp.eye(members, dtype=jnp.float32)
    factor = jnp.linalg.cholesky((members - 1.0) * unit_matrix[None] + gram)
    inverse = jax.vmap(
        lambda lower_f: jax.scipy.linalg.solve_triangular(lower_f, unit_matrix, lower=True)
    )(factor)
    scale = rho * jnp.sqrt(jnp.float32(members - 1.0))
    return scale[:, None, None] * jnp.swapaxes(inverse, 1, 2)


def local(anomalies, obs_cells, obs_counts, obs_precision, inflation):
    cell_width = anomalies.shape[2]
    members = anomalies.shape[3]
    slots = obs_cells.shape[1]
    first_cell = lax.axis_index("cell") * cell_width
    offsets = obs_cells - first_cell
    picked = jax.vmap(lambda field, where_at: field[0][where_at])(anomalies, offsets)
    live = jnp.arange(slots, dtype=jnp.int32)[None, :] < obs_counts
    picked = jnp.where(live[:, :, None], picked, jnp.zeros_like(picked))
    weights = jnp.where(live, obs_precision, jnp.float32(0.0))
    gathered, gathered_weights = (
        lax.all_gather(picked, "cell", axis=1, tiled=True),
        lax.all_gather(weights.astype(jnp.bfloat16), "cell", axis=1, tiled=True).astype(
            weights.dtype
        ),
    )
    gram = gram_of(gathered, gathered_weights)
    transforms = transform_of(gram, inflation)
    windows = transforms.shape[0]
    partial_list = [transforms[windows - 1]]
    for window in range(windows - 2, -1, -1):
        partial_list.insert(0, matmul_f32(transforms[window], partial_list[0]))
    own_product = partial_list[0]
    unit_matrix = jnp.eye(members, dtype=jnp.float32)
    products = lax.all_gather(
        own_product[None].astype(jnp.bfloat16), "tm", axis=0, tiled=True
    ).astype(jnp.float32)
    count = lax.axis_size("tm")
    position = lax.axis_index("tm")

    def absorb(turn, carried):
        source = count - 1 - turn
        updated = matmul_f32(products[source], carried)
        return jnp.where(source > position, updated, carried)

    later_product = lax.fori_loop(0, count, absorb, unit_matrix)
    suffixes = jnp.stack(
        [matmul_f32(partial_value, later_product) for partial_value in partial_list]
    )
    weight_mats = suffixes.astype(jnp.bfloat16)
    flat = anomalies.reshape(windows, 2 * cell_width, members)
    result = jnp.einsum("wcm,wmn->wcn", flat, weight_mats, preferred_element_type=jnp.float32)
    return result.astype(jnp.bfloat16).reshape(anomalies.shape)


def solution(mesh):
    placed = (
        P("tm", None, "cell", None),
        P("tm", "cell"),
        P("tm", "cell"),
        P("tm", "cell"),
        P("tm"),
    )
    return jax.shard_map(
        local, mesh=mesh, in_specs=placed, out_specs=P("tm", None, "cell", None), check_vma=False
    )
```

profile of v0, /device:TPU:0, one launch (start us, length us, event | category | flops | bytes accessed | tf_op | source)
XLA Modules:
  0.0 269.0 jit_solution(16111272196419085937)
XLA Ops:
  6.5 0.0 all-gather.4.cloned.1.call-start
  6.5 0.5 iota_multiply_fusion
  7.0 0.6 iota_compare_fusion.4
  7.7 0.6 iota_compare_fusion.3
  8.3 0.6 iota_compare_fusion.2
  8.9 0.8 fusion.21
  9.8 0.7 iota_compare_fusion.5
  10.5 0.7 broadcast_multiply_fusion
  11.2 0.8 fusion.35
  11.9 0.7 fusion.34
  12.6 0.1 reshape.87
  12.7 12.6 %all-gather.1 = bf16[4,32,3]{1,2,0:T(4,128)(2,1)S(1)} all-gather(bf16[1,32,3]{1,2,0:T(4,128)(2,1)S(1)} %fusion.35), channel_id=1, replica_groups=mesh['tm'=8,'cell'=4] {'cell'}, dimensions={0}, use_global_device_ids=true | all-gather | bytes 960 | tf_op jit(solution)/shard_map/all_gather | solution.py:46
  25.3 0.1 reshape.102
  25.4 0.7 fusion.38
  26.1 2.1 slice_bitcast_fusion
  28.2 2.2 gather_fusion
  30.4 0.9 broadcast_select_fusion
  31.3 13.6 %all_gather.9 = bf16[3,128,256]{2,1,0:T(8,128)(2,1)S(1)} all-gather(bf16[3,32,256]{2,1,0:T(8,128)(2,1)S(1)} %broadcast_select_fusion), channel_id=1, replica_groups=mesh['tm'=8,'cell'=4] {'cell'}, dimensions={1}, use_global_device_ids=true | all-gather | bytes 245760 | tf_op jit(solution)/shard_map/all_gather | solution.py:45
  44.9 0.6 fusion.15
  45.5 0.0 copy-start
  45.5 0.3 copy.52
  45.7 1.2 fusion.9
  46.9 35.2 %custom-call.17 = f32[3,128,128]{2,1,0:T(8,128)S(1)} custom-call(f32[3,128,128]{2,1,0:T(8,128)S(1)} %cholesky.122), custom_call_target="Cholesky" | custom-call | tf_op jit(solution)/shard_map/jit(cholesky)/cholesky | solution.py:26
  82.1 0.0 copy-done.3
  82.1 29.5 %custom-call.18 = f32[3,1,128,128]{2,3,1,0:T(8,128)S(1)} custom-call(f32[3,1,128,128]{3,2,1,0:T(8,128)S(1)} %select_bitcast_fusion), custom_call_target="InvertDiagBlocksLowerTriangular" | custom-call | tf_op jit(solution)/shard_map/jit(cholesky)/cholesky | solution.py:26
  111.6 0.1 cholesky.117
  111.7 0.4 constant_dynamic-update-slice_fusion.1
  112.1 0.5 convolution_subtract_fusion.1
  112.6 35.2 %custom-call.19 = f32[3,128,128]{2,1,0:T(8,128)S(1)} custom-call(f32[3,128,128]{2,1,0:T(8,128)S(1)} %convolution_subtract_fusion.1), custom_call_target="Cholesky" | custom-call | tf_op jit(solution)/shard_map/jit(cholesky)/cholesky | solution.py:26
  147.8 0.0 copy-done.2
  147.8 0.1 compare_reduce_fusion
  148.0 0.1 compare_reduce_fusion.1
  148.1 0.0 copy-done.1
  148.1 0.2 select_select_fusion
  148.3 0.1 triangular_solve.74
  148.3 5.4 %while.17 = (s32[]{:T(128)}, f32[3,256,256]{2,1,0:T(8,128)S(1)}, s32[2,2]{1,0:T(2,128)S(1)}, f32[2,3,128,128]{3,2,0,1:T(8,128)}, s32[]{:T(128)}) while((s32[]{:T(128)}, f32[3,256,256]{2,1,0:T(8,128)S(1)}, s32[2,2]{1,0:T(2,128)S(1)}, f32[2,3,128,128]{3,2,0,1:T(8,128)}, s32[]{:T(128)}) %tuple.56), condition=%wide.while_cond, body=%wide.while_body.sunk | while | flops 2 | bytes 394349 | solution.py:28
  148.3 0.6 fusion.58
  148.9 2.1 bitcast_dynamic-update-slice_fusion.2
  151.0 0.6 fusion.58
  151.6 2.1 bitcast_dynamic-update-slice_fusion.2
  153.7 59.8 %custom-call.20 = f32[3,2,128,128]{2,3,1,0:T(8,128)S(1)} custom-call(f32[3,2,128,128]{3,2,1,0:T(8,128)} %bitcast.105), custom_call_target="InvertDiagBlocksLowerTriangular" | custom-call | tf_op jit(solution)/shard_map/vmap(jit(_solve_triangular))/triangular_solve | solution.py:28
  213.5 0.5 fusion.25
  214.1 0.5 convolution_subtract_fusion
  214.5 0.5 fusion.24
  215.1 0.1 fusion.7
  215.2 0.6 fusion.18
  215.8 1.3 fusion.39
  217.1 0.0 all-gather.4.cloned.1.call-update
  217.2 21.8 %all-gather.4.cloned.1.call-done = bf16[2048,256]{1,0:T(8,128)(2,1)} async-done(((bf16[256,256]{1,0:T(8,128)(2,1)}), bf16[2048,256]{1,0:T(8,128)(2,1)}) %all-gather.4.cloned.1.call-update) | async-done | bytes 1048592 | tf_op jit(solution)/shard_map/all_gather | solution.py:58
  238.9 1.4 convert.15
  240.4 3.5 %while.16 = (s32[]{:T(128)}, f32[256,256]{1,0:T(8,128)S(1)}, s32[]{:T(128)}, f32[8,256,256]{2,1,0:T(8,128)S(1)}, s32[]{:T(128)}, /*index=5*/s32[]{:T(128)}, s32[]{:T(128)}, s32[]{:T(128)}) while((s32[]{:T(128)}, f32[256,256]{1,0:T(8,128)S(1)}, s32[]{:T(128)}, f32[8,256,256]{2,1,0:T(8,128)S(1)}, s32[]{:T(128)}, /*index=5*/s32[]{:T(128)}, ...), condition=%wide.region_5.6_spmd, body=%wide.region_4.5_spmd.sunk | while | flops 201392128 | bytes 1573017 | solution.py:69
  240.4 0.4 convolution_select_fusion.2
  240.9 0.4 convolution_select_fusion.2
  241.3 0.4 convolution_select_fusion.2
  241.7 0.4 convolution_select_fusion.2
  242.2 0.4 convolution_select_fusion.2
  242.6 0.4 convolution_select_fusion.2
  243.1 0.4 convolution_select_fusion.2
  243.5 0.4 convolution_select_fusion.2
  243.9 0.6 fusion.6
  244.5 0.4 fusion.5
  244.9 1.3 fusion.4
  246.2 7.3 %fusion.3 = bf16[3,4096,256]{1,2,0:T(8,128)(2,1)} fusion(bf16[3,4096,256]{2,1,0:T(8,128)(2,1)} %bitcast.99, bf16[1,256,256]{2,1,0:T(8,128)(2,1)S(1)} %fusion.6, bf16[1,256,256]{2,1,0:T(8,128)(2,1)S(1)} %fusion.5, bf16[1,256,256]{2,1,0:T(8,128)(2,1)S(1)} %fusion.4), kind=kOutput, calls=%fused_computation.8 | convolution fusion | flops 1614151680 | bytes 12976128 | tf_op jit(solution)/shard_map/wcm,wmn->wcn/dot_general | solution.py:75
  253.5 8.6 %copy.65 = bf16[3,4096,256]{2,1,0:T(8,128)(2,1)} copy(bf16[3,4096,256]{1,2,0:T(8,128)(2,1)} %fusion.3) | data formatting | bytes 12582912 | tf_op jit(solution)/shard_map/reshape | solution.py:76
  (23 shorter events, 0.3 us)
Async XLA Ops:
  6.5 232.4 %all-gather.4.cloned.1.call-start = ((), (), s32[]{:S(2)}) async-start(), calls=%async_computation | async-start | bytes 1179648 | tf_op jit(solution)/shard_map/all_gather | solution.py:58
  30.3 51.8 %copy-start.3 = (pred[128,128]{1,0:T(8,128)(4,1)S(1)}, pred[128,128]{1,0:T(8,128)(4,1)}, u32[]{:S(2)}) copy-start(pred[128,128]{1,0:T(8,128)(4,1)} %iota_compare_fusion.3) | copy-start | bytes 49156
  30.3 117.4 %copy-start.2 = (pred[128,128]{1,0:T(8,128)(4,1)S(1)}, pred[128,128]{1,0:T(8,128)(4,1)}, u32[]{:S(2)}) copy-start(pred[128,128]{1,0:T(8,128)(4,1)} %iota_compare_fusion.4) | copy-start | bytes 49156
  30.4 117.7 %copy-start.1 = (pred[256,256]{1,0:T(8,128)(4,1)S(1)}, pred[256,256]{1,0:T(8,128)(4,1)}, u32[]{:S(2)}) copy-start(pred[256,256]{1,0:T(8,128)(4,1)} %iota_compare_fusion.2) | copy-start | bytes 196612
  30.4 117.9 %copy-start.4 = (s32[2]{0:T(128)S(1)}, s32[2]{0:T(128)}, u32[]{:S(2)}) copy-start(s32[2]{0:T(128)} %iota_multiply_fusion) | copy-start | bytes 28
  45.5 168.1 %copy-start = (f32[128,256]{1,0:T(8,128)S(1)}, f32[128,256]{1,0:T(8,128)}, u32[]{:S(2)}) copy-start(f32[128,256]{1,0:T(8,128)} %get-tuple-element.145) | copy-start | bytes 393220
Sparse Core Ops, SparseCore 0:
  217.3 21.6 all-gather.3
where the time goes:
time: 270 us; the launch traced here: 269 us
  other arithmetic  170 us (63%)
  blocking collectives  26.2 us (10%)
  waiting for transfers between devices  21.8 us (8%)
  local copies, waits for them, and re-layouts  19.6 us (7%)
  matrix products  17.6 us (7%)
  between operations  13.6 us (5%)
    another operation x10, other arithmetic, transform_of(): factor = jnp.linalg.cholesky((members - 1.0) * unit_matrix[None] + gram)  101 us
    another operation x4, other arithmetic, transform_of(): jax.scipy.linalg.solve_triangular(lower_f, unit_matrix, lower=True)  61.1 us
    all_gather x1, waiting for transfers between devices, local(): lax.all_gather(own_product[None].astype(jnp.bfloat16), 'tm', axis=0, tile...  21.8 us
    all_gather x1, blocking collectives, local(): lax.all_gather(picked, 'cell', axis=1, tiled=True)  13.6 us
    all_gather x1, blocking collectives, local(): lax.all_gather(weights.astype(jnp.bfloat16), 'cell', axis=1, tiled=True)  12.6 us
    reshape x1, local copies, waits for them, and re-layouts, local(): return result.astype(jnp.bfloat16).reshape(anomalies.shape)  8.6 us
    dot_general x13, matrix products, matmul_f32(): jnp.dot(left, right, precision=lax.Precision.HIGHEST, preferred_element_t...  7.3 us
    dot_general x1, matrix products, local(): jnp.einsum('wcm,wmn->wcn', flat, weight_mats, preferred_element_type=jnp....  7.3 us
  transfers between devices with their start and end apart: 1, of which 1 were waited for; matrix products, arithmetic and copies ran while one was open for 0% of the time, Pallas kernels for 0%

commit v1 on v0

--- a/solution.py
+++ b/solution.py
@@ -55,8 +55,11 @@
         partial_list.insert(0, matmul_f32(transforms[window], partial_list[0]))
     own_product = partial_list[0]
     unit_matrix = jnp.eye(members, dtype=jnp.float32)
-    products = lax.all_gather(
-        own_product[None].astype(jnp.bfloat16), "tm", axis=0, tiled=True
+    products = jnp.concatenate(
+        lax.all_to_all(
+            jnp.stack([own_product[None].astype(jnp.bfloat16)] * lax.axis_size("tm")), "tm", 0, 0
+        ),
+        axis=0,
     ).astype(jnp.float32)
     count = lax.axis_size("tm")
     position = lax.axis_index("tm")

time: 270 us -> 255 us (0.944)
  between operations: 13.6 us -> 0.25 us
  waiting for transfers between devices: 21.8 us -> 15.4 us
  starting transfers between devices: 0.01 us -> 4.24 us
    all_gather x1 -> x0, waiting for transfers between devices: 21.8 us -> none  [local(): lax.all_gather(own_product[None].astype(jnp.bfloat16), 'tm', axis=0, tile...]
    all_to_all x0 -> x1, waiting for transfers between devices: none -> 15.4 us  [local(): lax.all_to_all(jnp.stack([own_product[None].astype(jnp.bfloat16)] * lax.a...]
    all_to_all x0 -> x1, starting transfers between devices: none -> 4.24 us  [local(): lax.all_to_all(jnp.stack([own_product[None].astype(jnp.bfloat16)] * lax.a...]
    another operation x6 -> x7, local copies, waits for them, and re-layouts: 5.39 us -> 6.39 us
where the time goes in v1:
time: 255 us; the launch traced here: 254 us
  other arithmetic  170 us (67%)
  blocking collectives  26.2 us (10%)
  local copies, waits for them, and re-layouts  20.6 us (8%)
  matrix products  17.5 us (7%)
  waiting for transfers between devices  15.4 us (6%)
  starting transfers between devices  4.24 us (2%)
    another operation x10, other arithmetic, transform_of(): factor = jnp.linalg.cholesky((members - 1.0) * unit_matrix[None] + gram)  101 us
    another operation x4, other arithmetic, transform_of(): jax.scipy.linalg.solve_triangular(lower_f, unit_matrix, lower=True)  61.1 us
    all_to_all x1, waiting for transfers between devices, local(): lax.all_to_all(jnp.stack([own_product[None].astype(jnp.bfloat16)] * lax.a...  15.4 us
    all_gather x1, blocking collectives, local(): lax.all_gather(picked, 'cell', axis=1, tiled=True)  13.6 us
    all_gather x1, blocking collectives, local(): lax.all_gather(weights.astype(jnp.bfloat16), 'cell', axis=1, tiled=True)  12.6 us
    reshape x1, local copies, waits for them, and re-layouts, local(): return result.astype(jnp.bfloat16).reshape(anomalies.shape)  8.6 us
    dot_general x1, matrix products, local(): jnp.einsum('wcm,wmn->wcn', flat, weight_mats, preferred_element_type=jnp....  7.29 us
    dot_general x13, matrix products, matmul_f32(): jnp.dot(left, right, precision=lax.Precision.HIGHEST, preferred_element_t...  7.27 us
  transfers between devices with their start and end apart: 1, of which 1 were waited for; matrix products, arithmetic and copies ran while one was open for 0% of the time, Pallas kernels for 0%

profile of v1, /device:TPU:0, one launch (start us, length us, event | category | flops | bytes accessed | tf_op | source)
XLA Modules:
  0.0 254.4 jit_solution(18238877953085504274)
XLA Ops:
  0.0 0.6 iota_multiply_fusion
  0.6 0.6 iota_compare_fusion.4
  1.2 0.6 iota_compare_fusion.3
  1.8 0.6 iota_compare_fusion.2
  2.5 0.8 fusion.21
  3.3 0.7 iota_compare_fusion.5
  4.0 0.7 broadcast_multiply_fusion
  4.7 0.8 fusion.35
  5.4 0.7 fusion.34
  6.1 0.1 reshape.94
  6.2 12.6 %all-gather = bf16[4,32,3]{1,2,0:T(4,128)(2,1)S(1)} all-gather(bf16[1,32,3]{1,2,0:T(4,128)(2,1)S(1)} %fusion.35), channel_id=1, replica_groups=mesh['tm'=8,'cell'=4] {'cell'}, dimensions={0}, use_global_device_ids=true | all-gather | bytes 960 | tf_op jit(solution)/shard_map/all_gather | solution.py:46
  18.9 0.1 reshape.107
  18.9 0.7 fusion.38
  19.6 2.1 slice_bitcast_fusion
  21.7 2.2 gather_fusion
  23.9 0.9 broadcast_select_fusion
  24.8 13.6 %all_gather.6 = bf16[3,128,256]{2,1,0:T(8,128)(2,1)S(1)} all-gather(bf16[3,32,256]{2,1,0:T(8,128)(2,1)S(1)} %broadcast_select_fusion), channel_id=1, replica_groups=mesh['tm'=8,'cell'=4] {'cell'}, dimensions={1}, use_global_device_ids=true | all-gather | bytes 245760 | tf_op jit(solution)/shard_map/all_gather | solution.py:45
  38.4 0.6 fusion.15
  39.0 0.0 copy-start
  39.0 0.3 copy.52
  39.2 1.2 fusion.9
  40.4 35.2 %custom-call.17 = f32[3,128,128]{2,1,0:T(8,128)S(1)} custom-call(f32[3,128,128]{2,1,0:T(8,128)S(1)} %cholesky.122), custom_call_target="Cholesky" | custom-call | tf_op jit(solution)/shard_map/jit(cholesky)/cholesky | solution.py:26
  75.6 0.0 copy-done.3
  75.6 29.5 %custom-call.18 = f32[3,1,128,128]{2,3,1,0:T(8,128)S(1)} custom-call(f32[3,1,128,128]{3,2,1,0:T(8,128)S(1)} %select_bitcast_fusion), custom_call_target="InvertDiagBlocksLowerTriangular" | custom-call | tf_op jit(solution)/shard_map/jit(cholesky)/cholesky | solution.py:26
  105.1 0.1 cholesky.117
  105.2 0.4 constant_dynamic-update-slice_fusion.1
  105.6 0.5 convolution_subtract_fusion.1
  106.1 35.2 %custom-call.19 = f32[3,128,128]{2,1,0:T(8,128)S(1)} custom-call(f32[3,128,128]{2,1,0:T(8,128)S(1)} %convolution_subtract_fusion.1), custom_call_target="Cholesky" | custom-call | tf_op jit(solution)/shard_map/jit(cholesky)/cholesky | solution.py:26
  141.3 0.1 compare_reduce_fusion
  141.5 0.1 compare_reduce_fusion.1
  141.6 0.0 copy-done.1
  141.6 0.2 select_select_fusion
  141.8 0.1 triangular_solve.74
  141.8 5.4 %while.17 = (s32[]{:T(128)}, f32[3,256,256]{2,1,0:T(8,128)S(1)}, s32[2,2]{1,0:T(2,128)S(1)}, f32[2,3,128,128]{3,2,0,1:T(8,128)}, s32[]{:T(128)}) while((s32[]{:T(128)}, f32[3,256,256]{2,1,0:T(8,128)S(1)}, s32[2,2]{1,0:T(2,128)S(1)}, f32[2,3,128,128]{3,2,0,1:T(8,128)}, s32[]{:T(128)}) %tuple.56), condition=%wide.while_cond, body=%wide.while_body.sunk | while | flops 2 | bytes 394349 | solution.py:28
  141.8 0.6 fusion.58
  142.5 2.1 bitcast_dynamic-update-slice_fusion.2
  144.5 0.6 fusion.58
  145.1 2.1 bitcast_dynamic-update-slice_fusion.2
  147.2 59.8 %custom-call.20 = f32[3,2,128,128]{2,3,1,0:T(8,128)S(1)} custom-call(f32[3,2,128,128]{3,2,1,0:T(8,128)} %bitcast.105), custom_call_target="InvertDiagBlocksLowerTriangular" | custom-call | tf_op jit(solution)/shard_map/vmap(jit(_solve_triangular))/triangular_solve | solution.py:28
  207.0 0.0 copy-done
  207.0 0.5 fusion.25
  207.5 0.5 convolution_subtract_fusion
  208.0 0.5 fusion.24
  208.5 0.1 fusion.7
  208.7 0.6 fusion.18
  209.3 1.3 fusion.39
  210.6 1.0 stack.27
  211.6 4.2 %all-to-all-start = ((bf16[8,1,256,256]{3,2,1,0:T(8,128)(2,1)}), bf16[8,1,256,256]{3,2,1,0:T(8,128)(2,1)}, u32[]{:S(2)}, u32[]{:S(2)}) async-start(bf16[8,1,256,256]{3,2,1,0:T(8,128)(2,1)} %stack.27), calls=%async_computation | async-start | bytes 2097152 | tf_op jit(solution)/shard_map/all_to_all | solution.py:59
  215.9 15.4 %all-to-all-done = bf16[8,1,256,256]{3,2,1,0:T(8,128)(2,1)} async-done(((bf16[8,1,256,256]{3,2,1,0:T(8,128)(2,1)}), bf16[8,1,256,256]{3,2,1,0:T(8,128)(2,1)}, u32[]{:S(2)}, u32[]{:S(2)}) %all-to-all-start) | async-done | bytes 1048608 | tf_op jit(solution)/shard_map/all_to_all | solution.py:59
  231.2 1.4 bitcast_convert_fusion
  232.7 3.5 %while.16 = (s32[]{:T(128)}, f32[256,256]{1,0:T(8,128)S(1)}, s32[]{:T(128)}, f32[8,256,256]{2,1,0:T(8,128)S(1)}, s32[]{:T(128)}, /*index=5*/s32[]{:T(128)}, s32[]{:T(128)}, s32[]{:T(128)}) while((s32[]{:T(128)}, f32[256,256]{1,0:T(8,128)S(1)}, s32[]{:T(128)}, f32[8,256,256]{2,1,0:T(8,128)S(1)}, s32[]{:T(128)}, /*index=5*/s32[]{:T(128)}, ...), condition=%wide.region_5.6_spmd, body=%wide.region_4.5_spmd.sunk | while | flops 201392128 | bytes 1573017 | solution.py:72
  232.7 0.4 convolution_select_fusion.2
  233.2 0.4 convolution_select_fusion.2
  233.6 0.4 convolution_select_fusion.2
  234.0 0.4 convolution_select_fusion.2
  234.5 0.4 convolution_select_fusion.2
  234.9 0.4 convolution_select_fusion.2
  235.4 0.4 convolution_select_fusion.2
  235.8 0.4 convolution_select_fusion.2
  236.2 0.6 fusion.6
  236.8 0.4 fusion.5
  237.2 1.3 fusion.4
  238.5 7.3 %fusion.3 = bf16[3,4096,256]{1,2,0:T(8,128)(2,1)} fusion(bf16[3,4096,256]{2,1,0:T(8,128)(2,1)} %bitcast.100, bf16[1,256,256]{2,1,0:T(8,128)(2,1)S(1)} %fusion.6, bf16[1,256,256]{2,1,0:T(8,128)(2,1)S(1)} %fusion.5, bf16[1,256,256]{2,1,0:T(8,128)(2,1)S(1)} %fusion.4), kind=kOutput, calls=%fused_computation.8 | convolution fusion | flops 1614151680 | bytes 12976128 | tf_op jit(solution)/shard_map/wcm,wmn->wcn/dot_general | solution.py:78
  245.8 8.6 %copy.65 = bf16[3,4096,256]{2,1,0:T(8,128)(2,1)} copy(bf16[3,4096,256]{1,2,0:T(8,128)(2,1)} %fusion.3) | data formatting | bytes 12582912 | tf_op jit(solution)/shard_map/reshape | solution.py:79
  (23 shorter events, 0.3 us)
Async XLA Ops:
  23.8 51.8 %copy-start.3 = (pred[128,128]{1,0:T(8,128)(4,1)S(1)}, pred[128,128]{1,0:T(8,128)(4,1)}, u32[]{:S(2)}) copy-start(pred[128,128]{1,0:T(8,128)(4,1)} %iota_compare_fusion.3) | copy-start | bytes 49156
  23.9 117.4 %copy-start.2 = (pred[128,128]{1,0:T(8,128)(4,1)S(1)}, pred[128,128]{1,0:T(8,128)(4,1)}, u32[]{:S(2)}) copy-start(pred[128,128]{1,0:T(8,128)(4,1)} %iota_compare_fusion.4) | copy-start | bytes 49156
  23.9 117.7 %copy-start.1 = (pred[256,256]{1,0:T(8,128)(4,1)S(1)}, pred[256,256]{1,0:T(8,128)(4,1)}, u32[]{:S(2)}) copy-start(pred[256,256]{1,0:T(8,128)(4,1)} %iota_compare_fusion.2) | copy-start | bytes 196612
  23.9 117.9 %copy-start.4 = (s32[2]{0:T(128)S(1)}, s32[2]{0:T(128)}, u32[]{:S(2)}) copy-start(s32[2]{0:T(128)} %iota_multiply_fusion) | copy-start | bytes 28
  39.0 168.0 %copy-start = (f32[128,256]{1,0:T(8,128)S(1)}, f32[128,256]{1,0:T(8,128)}, u32[]{:S(2)}) copy-start(f32[128,256]{1,0:T(8,128)} %get-tuple-element.145) | copy-start | bytes 393220
  211.6 19.6 %all-to-all-start = ((bf16[8,1,256,256]{3,2,1,0:T(8,128)(2,1)}), bf16[8,1,256,256]{3,2,1,0:T(8,128)(2,1)}, u32[]{:S(2)}, u32[]{:S(2)}) async-start(bf16[8,1,256,256]{3,2,1,0:T(8,128)(2,1)} %stack.27), calls=%async_computation | async-start | bytes 2097152 | tf_op jit(solution)/shard_map/all_to_all | solution.py:59
